TPU v7x, 32 devices: a whole 2x2x4 slice. The times are simulated.
32 devices in a mesh: rows: 8 (over y, x, core), grp: 4 (over z).
Axes of the slice: x: 2, y: 2, z: 4, core: 2. Of those that a mesh axis runs over, the one named last changes fastest.
Arguments:
- matrix: bfloat16 [16384, 2048], P(('rows', 'grp')), may hold values from -0.09375 to 0.09375
- right_side: bfloat16 [16384, 128], P(('rows', 'grp')), may hold values from -6 to 6
- precond: bfloat16 [2048, 2048], replicated, may hold values from -1 to 3
- row_counts: int32 [32], P(('rows', 'grp')), may hold values from 64 to 512, as said below
Outputs:
- solution: float32 [2048, 128], P(None, 'grp')
- coeffs: float32 [2048, 128], P(None, 'grp')
- rel_residual: float32 [128], P('grp')
Inputs may be any that keep to these rules, and one draw needn't show every extreme that they name: Device d holds A's rows in its first row_counts[d] slots of 512; some device is full in every draw.
All inputs are finite; a program needn't handle non-finite values.
Results may differ from a plain program's by a relative error of at most 0.0128.
Values may be sent and summed in bfloat16 or wider, within the bound.
A program may use at most 64 MiB of HBM per device.

v0:
```python
import jax
import jax.numpy as jnp
from jax import lax
from jax.sharding import PartitionSpec as P

ITERS = 3


floor_sq = 0.01


def pull_partial(matrix, residue):
    partial_value = lax.dot_general(
        matrix,
        residue.astype(jnp.bfloat16),
        (((0,), (0,)), ((), ())),
        preferred_element_type=jnp.float32,
    )
    squares = jnp.sum(residue * residue, axis=0, keepdims=True)
    return (partial_value, squares)


def column_section(precond, partial_value, squares, right_vec):
    u_norm = jnp.sqrt(squares + floor_sq)
    pulled = lax.dot_general(
        precond,
        (partial_value / u_norm).astype(jnp.bfloat16),
        (((0,), (0,)), ((), ())),
        preferred_element_type=jnp.float32,
    )
    raw_vec = pulled - u_norm * right_vec
    v_norm = jnp.sqrt(jnp.sum(raw_vec * raw_vec, axis=0, keepdims=True) + floor_sq)
    return (u_norm, raw_vec / v_norm, v_norm)


def shards(matrix, right_side, precond, row_counts):
    local_rows, width = matrix.shape
    count = row_counts[0]
    live_rows = (lax.broadcasted_iota(jnp.int32, (local_rows, 1), 0) < count).astype(jnp.float32)

    def row_pass(pushed, v_norm_all, left_vec):
        if pushed is None:
            residue = live_rows * right_side.astype(jnp.float32)
        else:
            residue = live_rows * (
                jnp.dot(matrix, pushed, preferred_element_type=jnp.float32) - v_norm_all * left_vec
            )
        partial_value, squares = pull_partial(matrix, residue)
        return (residue, partial_value, squares)

    def reduce_cols(partial_value, squares):
        shared, shared_sq = (
            lax.psum_scatter(partial_value, "grp", scatter_dimension=1, tiled=True),
            lax.psum_scatter(squares, "grp", scatter_dimension=1, tiled=True),
        )
        return lax.psum((shared, shared_sq), "rows")

    def share_cols(right_vec, v_norm, u_norm):
        pushed = jnp.dot(
            precond, right_vec.astype(jnp.bfloat16), preferred_element_type=jnp.float32
        ).astype(jnp.bfloat16)
        pushed = lax.all_gather(pushed, "grp", axis=1, tiled=True)
        norms = lax.all_gather(jnp.concatenate([v_norm, u_norm], axis=0), "grp", axis=1, tiled=True)
        return (pushed, norms[0:1], norms[1:2])

    residue, partial_value, squares = row_pass(None, None, None)
    partial_value, squares = reduce_cols(partial_value, squares)
    u_norm, right_vec, v_norm = column_section(
        precond, partial_value, squares, jnp.zeros((width, partial_value.shape[1]), jnp.float32)
    )
    phi_bar = u_norm
    rho_bar = v_norm
    search = right_vec
    coeffs = jnp.zeros(right_vec.shape, jnp.float32)
    start_norm = u_norm
    pushed, v_norm_all, u_norm_all = share_cols(right_vec, v_norm, u_norm)
    left_vec = residue / u_norm_all
    for turn_index in range(ITERS):
        residue, partial_value, squares = row_pass(pushed, v_norm_all, left_vec)
        partial_value, squares = reduce_cols(partial_value, squares)
        u_norm, next_vec, next_norm = column_section(precond, partial_value, squares, right_vec)
        radius = jnp.sqrt(rho_bar * rho_bar + u_norm * u_norm)
        cosine = rho_bar / radius
        sine_part = u_norm / radius
        coupling = sine_part * next_norm
        rho_bar = -cosine * next_norm
        phi_step = cosine * phi_bar
        phi_bar = sine_part * phi_bar
        coeffs = coeffs + phi_step / radius * search
        search = next_vec - coupling / radius * search
        right_vec = next_vec
        v_norm = next_norm
        if turn_index + 1 < ITERS:
            pushed, v_norm_all, u_norm_all = share_cols(right_vec, v_norm, u_norm)
            left_vec = residue / u_norm_all
    ratio = phi_bar / start_norm
    solution = jnp.dot(precond, coeffs.astype(jnp.bfloat16), preferred_element_type=jnp.float32)
    return (solution, coeffs, ratio[0])


def solution(mesh):
    return jax.shard_map(
        shards,
        mesh=mesh,
        in_specs=(P(("rows", "grp"), None), P(("rows", "grp"), None), P(), P(("rows", "grp"))),
        out_specs=(P(None, "grp"), P(None, "grp"), P("grp")),
        check_vma=False,
    )
```

profile of v0, /device:TPU:0, one launch (start us, length us, event | category | flops | bytes accessed | tf_op | source)
XLA Modules:
  0.0 477.1 jit_solution(473941250615389567)
XLA Ops:
  7.2 0.0 reduce-scatter.22.cloned.1.call-start
  8.0 1.0 copy.12
  9.0 0.1 multiply_reduce_fusion.5
  9.2 0.7 copy.16
  9.9 0.0 reduce-scatter.22.cloned.1.call-update
  9.9 0.0 reduce-scatter.16.cloned.1.call-start
  10.0 1.4 convolution_bitcast_fusion.2
  11.5 0.0 all-reduce.4.cloned.1.call-start
  11.5 21.3 %reduce-scatter.22.cloned.1.call-done = f32[32,1]{1,0:T(8,128)} async-done(((f32[128,1]{1,0:T(8,128)}), f32[32,1]{1,0:T(8,128)}) %reduce-scatter.22.cloned.1.call-update) | async-done | bytes 144
  32.8 0.8 copy.17
  33.6 11.8 %psum.50 = f32[1,32]{1,0:T(1,128)S(1)} all-reduce(f32[1,32]{1,0:T(1,128)S(1)} %copy.17), channel_id=1, replica_groups=mesh['rows'=8,'grp'=4] {'rows'}, use_global_device_ids=true, to_apply=%region_4.0 | all-reduce | flops 32 | bytes 256 | tf_op jit(solution)/shard_map/psum | solution.py:56
  45.5 15.1 %reduce-scatter.16.cloned.1.call-done = f32[2048,32]{0,1:T(8,128)} async-done(((f32[2048,128]{0,1:T(8,128)}), f32[2048,32]{0,1:T(8,128)}) %reduce-scatter.16.cloned.1.call-update) | async-done | bytes 262160 | tf_op jit(solution)/shard_map/reduce_scatter | solution.py:53
  60.6 0.0 all-reduce.4.cloned.1.call-update
  60.6 0.0 reduce-scatter.24.cloned.1.call-start
  60.7 55.4 %all-reduce.4.cloned.1.call-done = f32[2048,32]{0,1:T(8,128)} async-done(((f32[2048,32]{0,1:T(8,128)}), f32[2048,32]{0,1:T(8,128)}) %all-reduce.4.cloned.1.call-update) | async-done | bytes 262160 | tf_op jit(solution)/shard_map/psum | solution.py:56
  116.1 5.2 %multiply_reduce_fusion.4 = (f32[32]{0:T(128)S(1)}, f32[32,2048]{1,0:T(8,128)S(1)}) fusion(f32[32]{0:T(128)S(1)} %broadcast_multiply_fusion, bf16[2048,2048]{1,0:T(8,128)(2,1)} %param.6, f32[2048,32]{0,1:T(8,128)} %all-reduce.4.cloned.1.call-done, f32[32]{0:T(128)S(1)} %get-tuple-element.32), kind=kOutput, calls=%fused_computation.31 | convolution fusion | flops 268763104 | bytes 8913280 | tf_op jit(solution)/shard_map/dot_general | solution.py:25
  121.3 6.0 %fusion = bf16[2048,32]{0,1:T(8,128)(2,1)S(1)} fusion(bf16[2048,2048]{1,0:T(8,128)(2,1)} %param.6, f32[32,2048]{1,0:T(8,128)S(1)} %get-tuple-element.34, f32[32]{0:T(128)S(1)} %get-tuple-element.30), kind=kOutput, calls=%fused_computation.10 | convolution fusion | flops 268632064 | bytes 8781952 | tf_op jit(solution)/shard_map/dot_general | solution.py:59
  127.3 14.9 %all_gather.18 = bf16[2048,128]{0,1:T(8,128)(2,1)S(1)} all-gather(bf16[2048,32]{0,1:T(8,128)(2,1)S(1)} %fusion), channel_id=1, replica_groups=mesh['rows'=8,'grp'=4] {'grp'}, dimensions={1}, use_global_device_ids=true | all-gather | bytes 655360 | tf_op jit(solution)/shard_map/all_gather | solution.py:62
  142.2 11.7 %all-gather = f32[4,32,2]{1,2,0:T(2,128)S(1)} all-gather(f32[1,32,2]{1,2,0:T(2,128)S(1)} %maximum_bitcast_fusion), channel_id=1, replica_groups=mesh['rows'=8,'grp'=4] {'grp'}, dimensions={0}, use_global_device_ids=true | all-gather | bytes 1280 | tf_op jit(solution)/shard_map/all_gather | solution.py:63
  153.9 0.1 reshape.67
  154.0 0.9 multiply_reduce_fusion.3
  154.9 0.8 copy.18
  155.7 0.0 reduce-scatter.24.cloned.1.call-update
  155.7 0.0 reduce-scatter.18.cloned.1.call-start
  155.8 1.4 convolution_bitcast_fusion.1
  157.2 0.0 all-reduce.6.cloned.1.call-start
  157.3 14.5 %reduce-scatter.24.cloned.1.call-done = f32[32,1]{1,0:T(8,128)} async-done(((f32[128,1]{1,0:T(8,128)}), f32[32,1]{1,0:T(8,128)}) %reduce-scatter.24.cloned.1.call-update) | async-done | bytes 144
  171.8 0.8 copy.19
  172.5 11.9 %psum.51 = f32[1,32]{1,0:T(1,128)S(1)} all-reduce(f32[1,32]{1,0:T(1,128)S(1)} %copy.19), channel_id=1, replica_groups=mesh['rows'=8,'grp'=4] {'rows'}, use_global_device_ids=true, to_apply=%region_8.0 | all-reduce | flops 32 | bytes 256 | tf_op jit(solution)/shard_map/psum | solution.py:56
  184.4 15.0 %reduce-scatter.18.cloned.1.call-done = f32[2048,32]{0,1:T(8,128)} async-done(((f32[2048,128]{0,1:T(8,128)}), f32[2048,32]{0,1:T(8,128)}) %reduce-scatter.18.cloned.1.call-update) | async-done | bytes 262160 | tf_op jit(solution)/shard_map/reduce_scatter | solution.py:53
  199.4 0.0 reduce-scatter.26.cloned.1.call-start
  199.5 55.2 %all-reduce.6.cloned.1.call-done = f32[2048,32]{0,1:T(8,128)} async-done(((f32[2048,32]{0,1:T(8,128)}), f32[2048,32]{0,1:T(8,128)}) %all-reduce.6.cloned.1.call-update) | async-done | bytes 262160 | tf_op jit(solution)/shard_map/psum | solution.py:56
  254.7 5.2 %multiply_reduce_fusion.1 = (f32[32]{0:T(128)S(1)}, f32[32,2048]{1,0:T(8,128)S(1)}) fusion(f32[32,2048]{1,0:T(8,128)S(1)} %get-tuple-element.34, f32[32]{0:T(128)S(1)} %get-tuple-element.30, f32[32]{0:T(128)S(1)} %get-tuple-element.28, bf16[2048,2048]{1,0:T(8,128)(2,1)} %param.6, f32[2048,32]{0,1:T(8,128)} %all-reduce.6.cloned.1.call-done), kind=kOutput, calls=%fused_computation.26 | convolution fusion | flops 268894176 | bytes 9175424 | tf_op jit(solution)/shard_map/dot_general | solution.py:25
  259.9 6.0 %fusion.1 = bf16[2048,32]{0,1:T(8,128)(2,1)S(1)} fusion(bf16[2048,2048]{1,0:T(8,128)(2,1)} %param.6, f32[32,2048]{1,0:T(8,128)S(1)} %get-tuple-element.38, f32[32]{0:T(128)S(1)} %get-tuple-element.26), kind=kOutput, calls=%fused_computation.11 | convolution fusion | flops 268632064 | bytes 8781952 | tf_op jit(solution)/shard_map/dot_general | solution.py:59
  265.9 14.9 %all_gather.20 = bf16[2048,128]{0,1:T(8,128)(2,1)S(1)} all-gather(bf16[2048,32]{0,1:T(8,128)(2,1)S(1)} %fusion.1), channel_id=1, replica_groups=mesh['rows'=8,'grp'=4] {'grp'}, dimensions={1}, use_global_device_ids=true | all-gather | bytes 655360 | tf_op jit(solution)/shard_map/all_gather | solution.py:62
  280.9 11.7 %all-gather.1 = f32[4,32,2]{1,2,0:T(2,128)S(1)} all-gather(f32[1,32,2]{1,2,0:T(2,128)S(1)} %maximum_bitcast_fusion.1), channel_id=1, replica_groups=mesh['rows'=8,'grp'=4] {'grp'}, dimensions={0}, use_global_device_ids=true | all-gather | bytes 1280 | tf_op jit(solution)/shard_map/all_gather | solution.py:63
  292.5 0.1 reshape.69
  292.6 1.5 multiply_reduce_fusion.2
  294.2 0.7 copy.20
  294.9 0.0 reduce-scatter.26.cloned.1.call-update
  295.0 0.0 reduce-scatter.20.cloned.1.call-start
  295.0 2.4 convolution_bitcast_fusion
  297.4 0.0 reduce-scatter.20.cloned.1.call-update
  297.4 0.0 all-reduce.8.cloned.1.call-start
  297.5 13.5 %reduce-scatter.26.cloned.1.call-done = f32[32,1]{1,0:T(8,128)} async-done(((f32[128,1]{1,0:T(8,128)}), f32[32,1]{1,0:T(8,128)}) %reduce-scatter.26.cloned.1.call-update) | async-done | bytes 144
  311.0 0.8 copy.21
  311.8 11.8 %psum.53 = f32[1,32]{1,0:T(1,128)S(1)} all-reduce(f32[1,32]{1,0:T(1,128)S(1)} %copy.21), channel_id=1, replica_groups=mesh['rows'=8,'grp'=4] {'rows'}, use_global_device_ids=true, to_apply=%region_14.0 | all-reduce | flops 32 | bytes 256 | tf_op jit(solution)/shard_map/psum | solution.py:56
  323.6 15.2 %reduce-scatter.20.cloned.1.call-done = f32[2048,32]{0,1:T(8,128)} async-done(((f32[2048,128]{0,1:T(8,128)}), f32[2048,32]{0,1:T(8,128)}) %reduce-scatter.20.cloned.1.call-update) | async-done | bytes 262160 | tf_op jit(solution)/shard_map/reduce_scatter | solution.py:53
  338.8 0.0 all-reduce.8.cloned.1.call-update
  338.8 0.0 reduce-scatter.28.cloned.1.call-start
  338.8 55.4 %all-reduce.8.cloned.1.call-done = f32[2048,32]{0,1:T(8,128)} async-done(((f32[2048,32]{0,1:T(8,128)}), f32[2048,32]{0,1:T(8,128)}) %all-reduce.8.cloned.1.call-update) | async-done | bytes 262160 | tf_op jit(solution)/shard_map/psum | solution.py:56
  394.2 5.2 %multiply_reduce_fusion = (f32[32]{0:T(128)S(1)}, f32[32,2048]{1,0:T(8,128)S(1)}) fusion(f32[32,2048]{1,0:T(8,128)S(1)} %get-tuple-element.38, f32[32]{0:T(128)S(1)} %get-tuple-element.26, f32[32]{0:T(128)S(1)} %get-tuple-element.24, bf16[2048,2048]{1,0:T(8,128)(2,1)} %param.6, f32[2048,32]{0,1:T(8,128)} %all-reduce.8.cloned.1.call-done), kind=kOutput, calls=%fused_computation.25 | convolution fusion | flops 268894176 | bytes 9175424 | tf_op jit(solution)/shard_map/dot_general | solution.py:25
  399.4 11.2 %all-gather.2 = f32[4,32,2]{1,2,0:T(2,128)S(1)} all-gather(f32[1,32,2]{1,2,0:T(2,128)S(1)} %maximum_bitcast_fusion.2), channel_id=1, replica_groups=mesh['rows'=8,'grp'=4] {'grp'}, dimensions={0}, use_global_device_ids=true | all-gather | bytes 1280 | tf_op jit(solution)/shard_map/all_gather | solution.py:63
  410.7 0.1 reshape.71
  410.8 6.0 %fusion.2 = bf16[2048,32]{0,1:T(8,128)(2,1)S(1)} fusion(bf16[2048,2048]{1,0:T(8,128)(2,1)} %param.6, f32[32,2048]{1,0:T(8,128)S(1)} %get-tuple-element.42, f32[32]{0:T(128)S(1)} %get-tuple-element.22), kind=kOutput, calls=%fused_computation.12 | convolution fusion | flops 268632064 | bytes 8781952 | tf_op jit(solution)/shard_map/dot_general | solution.py:59
  416.8 14.8 %all_gather.22 = bf16[2048,128]{0,1:T(8,128)(2,1)S(1)} all-gather(bf16[2048,32]{0,1:T(8,128)(2,1)S(1)} %fusion.2), channel_id=1, replica_groups=mesh['rows'=8,'grp'=4] {'grp'}, dimensions={1}, use_global_device_ids=true | all-gather | bytes 655360 | tf_op jit(solution)/shard_map/all_gather | solution.py:62
  431.5 0.9 fusion.10
  432.5 0.8 copy.22
  433.2 16.8 %reduce-scatter.28.cloned.1.call-done = f32[32,1]{1,0:T(8,128)} async-done(((f32[128,1]{1,0:T(8,128)}), f32[32,1]{1,0:T(8,128)}) %reduce-scatter.28.cloned.1.call-update) | async-done | bytes 144
  450.0 0.8 copy.23
  450.8 11.8 %psum.55 = f32[1,32]{1,0:T(1,128)S(1)} all-reduce(f32[1,32]{1,0:T(1,128)S(1)} %copy.23), channel_id=1, replica_groups=mesh['rows'=8,'grp'=4] {'rows'}, use_global_device_ids=true, to_apply=%region_20.0 | all-reduce | flops 32 | bytes 256 | tf_op jit(solution)/shard_map/psum | solution.py:56
  462.6 0.6 fusion.29
  463.2 0.2 add_bitcast_fusion
  463.4 6.8 %convolution_bitcast_fusion.3 = f32[2048,32]{0,1:T(8,128)} fusion(bf16[2048,2048]{1,0:T(8,128)(2,1)} %param.6, f32[2048,32]{0,1:T(8,128)S(1)} %add_bitcast_fusion), kind=kOutput, calls=%fused_computation.3 | convolution fusion | flops 268500992 | bytes 8912896 | tf_op jit(solution)/shard_map/dot_general | solution.py:97
  (28 shorter events, 0.2 us)
Async XLA Ops:
  7.2 2.8 copy-start
  7.2 25.6 %reduce-scatter.22.cloned.1.call-start = ((), (), s32[]{:S(2)}) async-start(), calls=%async_computation.13 | async-start | bytes 81920
  9.9 50.7 %reduce-scatter.16.cloned.1.call-start = ((), (), s32[]{:S(2)}) async-start(), calls=%async_computation.7 | async-start | bytes 1310720 | tf_op jit(solution)/shard_map/reduce_scatter | solution.py:53
  11.5 104.6 %all-reduce.4.cloned.1.call-start = ((), (), s32[]{:S(2)}) async-start(), calls=%async_computation.8 | async-start | bytes 524288 | tf_op jit(solution)/shard_map/psum | solution.py:56
  60.6 111.1 %reduce-scatter.24.cloned.1.call-start = ((), (), s32[]{:S(2)}) async-start(), calls=%async_computation.14 | async-start | bytes 81920
  155.7 43.7 %reduce-scatter.18.cloned.1.call-start = ((), (), s32[]{:S(2)}) async-start(), calls=%async_computation.9 | async-start | bytes 1310720 | tf_op jit(solution)/shard_map/reduce_scatter | solution.py:53
  157.2 97.5 %all-reduce.6.cloned.1.call-start = ((), (), s32[]{:S(2)}) async-start(), calls=%async_computation.10 | async-start | bytes 524288 | tf_op jit(solution)/shard_map/psum | solution.py:56
  199.4 111.5 %reduce-scatter.26.cloned.1.call-start = ((), (), s32[]{:S(2)}) async-start(), calls=%async_computation.15 | async-start | bytes 81920
  295.0 43.8 %reduce-scatter.20.cloned.1.call-start = ((), (), s32[]{:S(2)}) async-start(), calls=%async_computation.11 | async-start | bytes 1310720 | tf_op jit(solution)/shard_map/reduce_scatter | solution.py:53
  297.4 96.8 %all-reduce.8.cloned.1.call-start = ((), (), s32[]{:S(2)}) async-start(), calls=%async_computation.12 | async-start | bytes 524288 | tf_op jit(solution)/shard_map/psum | solution.py:56
  338.8 111.2 %reduce-scatter.28.cloned.1.call-start = ((), (), s32[]{:S(2)}) async-start(), calls=%async_computation.16 | async-start | bytes 81920
  399.4 32.1 %copy-start.2 = (f32[512,128]{0,1:T(8,128)S(1)}, f32[512,128]{0,1:T(8,128)}, u32[]{:S(2)}) copy-start(f32[512,128]{0,1:T(8,128)} %get-tuple-element.40) | copy-start | bytes 786436
  463.4 6.8 %copy-start.1 = (f32[2048,32]{0,1:T(8,128)}, f32[2048,32]{0,1:T(8,128)S(1)}, u32[]{:S(2)}) copy-start(f32[2048,32]{0,1:T(8,128)S(1)} %add_bitcast_fusion) | copy-start | bytes 786436
Sparse Core Ops, SparseCore 0:
  10.8 21.9 reduce-scatter.21
  35.1 25.4 reduce-scatter.15
  63.7 52.3 all-reduce.3
  155.8 15.8 reduce-scatter.23
  173.9 25.4 reduce-scatter.17
  202.3 52.3 all-reduce.5
  295.1 15.8 reduce-scatter.25
  313.3 25.4 reduce-scatter.19
  341.8 52.3 all-reduce.7
  433.4 16.6 reduce-scatter.27
where the time goes:
time: 478 us; the launch traced here: 477 us
  waiting for transfers between devices  278 us (58%)
  blocking collectives  127 us (27%)
  matrix products  49 us (10%)
  between operations  15.1 us (3%)
  local copies, waits for them, and re-layouts  7.48 us (2%)
    psum x3, waiting for transfers between devices, reduce_cols(): return lax.psum((shared, shared_sq), 'rows')  166 us
    unnamed x14, waiting for transfers between devices  66.2 us
    psum x4, blocking collectives, reduce_cols(): return lax.psum((shared, shared_sq), 'rows')  47.4 us
    reduce_scatter x3, waiting for transfers between devices, reduce_cols(): lax.psum_scatter(partial_value, 'grp', scatter_dimension=1, tiled=True)  45.3 us
    all_gather x3, blocking collectives, share_cols(): pushed = lax.all_gather(pushed, 'grp', axis=1, tiled=True)  44.6 us
    all_gather x3, blocking collectives, share_cols(): lax.all_gather(jnp.concatenate([v_norm, u_norm], axis=0), 'grp', axis=1,...  34.6 us
    dot_general x3, matrix products, share_cols(): jnp.dot(precond, right_vec.astype(jnp.bfloat16), preferred_element_type=j...  18 us
    dot_general x3, matrix products, column_section(): lax.dot_general(precond, (partial_value / u_norm).astype(jnp.bfloat16), (...  15.6 us
  transfers between devices with their start and end apart: 10, of which 10 were waited for; matrix products, arithmetic and copies ran while one was open for 2% of the time, Pallas kernels for 0%

commit v1 on v0

v1 whole, which is shorter than its diff:
```python
import functools

import jax
import jax.numpy as jnp
from jax import lax
from jax.experimental import pallas as pl
from jax.experimental.pallas import tpu as pltpu
from jax.sharding import PartitionSpec as P

ITERS = 3
CORES = 2
FLOOR_SQ = 0.01
F32 = jnp.float32
BF16 = jnp.bfloat16
MESH = pl.DeviceIdType.MESH


def body(
    nxy, nz,
    count_ref, a_hbm, b_ref, n_hbm,
    sol_ref, coef_ref, ratio_ref,
    a_ref, n_ref, c_ref, ct_ref, left_ref, vecs_ref, pb_ref, vb_ref, ft_ref, w_ref, nw_ref,
    tx0, rx0, hbuf, tx1, rx1, tx2, rx2, full,
    sqtx, sqrx0, sqrx1, sqrx2,
    load_sem, s0, r0, s1, r1, s2, r2, gs2, gr2, gs1, gr1, gs0, gr0,
    qs0, qr0, qs1, qr1, qs2, qr2,
):
    row = lax.axis_index("rows")
    z = lax.axis_index("grp")
    core = lax.rem(row, CORES)
    xy = row // CORES
    other = 1 - core
    local, width = a_ref.shape
    cols = b_ref.shape[1]
    chunk = full.shape[3]
    group = nxy * chunk
    own_cols = cols // nz

    def xy_peer(k):
        return lax.rem(xy + k, nxy)

    def z_peer(k):
        return lax.rem(z + k, nz)

    def row_id(at):
        return {"rows": at * CORES + core}

    core_id = {"rows": xy * CORES + other}

    load_a = pltpu.make_async_copy(a_hbm, a_ref, load_sem.at[0])
    load_n = pltpu.make_async_copy(n_hbm, n_ref, load_sem.at[1])
    load_a.start()
    load_n.start()

    barrier = pltpu.get_barrier_semaphore()
    pl.semaphore_signal(barrier, inc=1, device_id=core_id, device_id_type=MESH)
    for k in range(1, nxy):
        pl.semaphore_signal(barrier, inc=1, device_id=row_id(xy_peer(k)), device_id_type=MESH)
    for k in range(1, nz):
        pl.semaphore_signal(barrier, inc=1, device_id={"grp": z_peer(k)}, device_id_type=MESH)

    def remote(src, dst, ssem, rsem, to):
        copy = pltpu.make_async_remote_copy(
            src_ref=src, dst_ref=dst, send_sem=ssem, recv_sem=rsem, device_id=to, device_id_type=MESH
        )
        copy.start()
        return copy

    def flat(value):
        return value.astype(F32).reshape(-1, cols)

    def pieces(value):
        return value.reshape(-1, chunk, cols).astype(BF16)

    class Squares:
        def __init__(self, turn, local_sq):
            self.turn = turn
            self.total = jnp.broadcast_to(local_sq, (8, cols))
            self.sent = []

        def send_core(self):
            sqtx[self.turn, 0] = self.total
            self.now = [remote(sqtx.at[self.turn, 0], sqrx0.at[self.turn], qs0.at[self.turn], qr0.at[self.turn], core_id)]

        def send_xy(self):
            self.now[0].wait_recv()
            self.sent += self.now
            self.total = self.total + sqrx0[self.turn]
            sqtx[self.turn, 1] = self.total
            sqrx1[self.turn, xy] = self.total
            self.now = [
                remote(sqtx.at[self.turn, 1], sqrx1.at[self.turn, xy], qs1.at[self.turn, k - 1], qr1.at[self.turn, k - 1], row_id(xy_peer(k)))
                for k in range(1, nxy)
            ]

        def send_z(self):
            for copy in self.now:
                copy.wait_recv()
            self.sent += self.now
            self.total = sum(sqrx1[self.turn, at] for at in range(nxy))
            sqtx[self.turn, 2] = self.total
            sqrx2[self.turn, z] = self.total
            self.now = [
                remote(sqtx.at[self.turn, 2], sqrx2.at[self.turn, z], qs2.at[self.turn, k - 1], qr2.at[self.turn, k - 1], {"grp": z_peer(k)})
                for k in range(1, nz)
            ]

        def finish(self):
            for copy in self.now:
                copy.wait_recv()
            self.sent += self.now
            self.total = sum(sqrx2[self.turn, at] for at in range(nz))
            for copy in self.sent:
                copy.wait_send()
            return self.total[0:1]

    def all_reduce(turn, product, local_sq, filler):
        order = list(range(1, nz)) + [0]
        sends = []
        core_copies = {}
        for d in order:
            s = z_peer(d)
            tx0[s] = pieces(product(other, s))
            core_copies[d] = remote(tx0.at[s], rx0.at[s], s0.at[d], r0.at[d], core_id)
        squares = Squares(turn, local_sq)
        squares.send_core()
        for d in order:
            s = z_peer(d)
            hbuf[s] = product(core, s).reshape(nxy, chunk, cols)
        xy_copies = {}
        for d in order:
            s = z_peer(d)
            core_copies[d].wait_recv()
            total = hbuf[s] + rx0[s].astype(F32)
            hbuf[s] = total
            tx1[s] = total.astype(BF16)
            for k in range(1, nxy):
                at = xy_peer(k)
                xy_copies[d, k] = remote(
                    tx1.at[s, at], rx1.at[d, k - 1], s1.at[d, k - 1], r1.at[d, k - 1], row_id(at)
                )
        squares.send_xy()
        filler(2)
        z_copies = {}
        for d in order:
            s = z_peer(d)
            part = hbuf[s, xy]
            for k in range(1, nxy):
                xy_copies[d, k].wait_recv()
                part = part + rx1[d, k - 1].astype(F32)
            if d:
                tx2[d - 1] = part.astype(BF16)
                z_copies[d] = remote(
                    tx2.at[d - 1], rx2.at[d - 1], s2.at[d - 1], r2.at[d - 1], {"grp": s}
                )
        squares.send_z()
        filler(2)
        for d in range(1, nz):
            z_copies[d].wait_recv()
            part = part + rx2[d - 1].astype(F32)
        full[core, z, xy] = part.astype(BF16)
        gather_z = [
            remote(full.at[core, z, xy], full.at[core, z, xy], gs2.at[d - 1], gr2.at[d - 1], {"grp": z_peer(d)})
            for d in range(1, nz)
        ]
        gather_xy = {}

        def spread(d, zz):
            for k in range(1, nxy):
                gather_xy[d, k] = remote(
                    full.at[core, zz, xy], full.at[core, zz, xy],
                    gs1.at[d, k - 1], gr1.at[d, k - 1], row_id(xy_peer(k)),
                )

        spread(0, z)
        total_sq = squares.finish()
        filler(3)
        for d in range(1, nz):
            gather_z[d - 1].wait_recv()
            spread(d, z_peer(nz - d))
        filler(1)
        gather_core = []
        for d in range(nz):
            zz = z_peer((nz - d) % nz)
            for k in range(1, nxy):
                gather_xy[d, k].wait_recv()
            gather_core.append(
                remote(full.at[core, zz], full.at[core, zz], gs0.at[d], gr0.at[d], core_id)
            )
        for copy in gather_core:
            copy.wait_recv()
        for copies in (core_copies, xy_copies, z_copies, gather_xy):
            for copy in copies.values():
                copy.wait_send()
        for copy in gather_z + gather_core:
            copy.wait_send()
        return total_sq

    live = (lax.broadcasted_iota(jnp.int32, (local, 1), 0) < count_ref[0]).astype(F32)

    residue = live * b_ref[...].astype(F32)
    left_ref[...] = residue
    sq = jnp.sum(residue * residue, axis=0, keepdims=True)
    bt = residue.T.astype(BF16)
    pl.semaphore_wait(barrier, nxy + nz - 1)
    load_a.wait()

    def first_product(half, s):
        start = pl.multiple_of((half * nz + s) * group, group)
        return jnp.dot(bt, a_ref[:, pl.ds(start, group)], preferred_element_type=F32).T

    block = 256
    todo = list(range(width // block))

    def form_c(times):
        if len(todo) == width // block:
            load_n.wait()
        for _ in range(times):
            if todo:
                at = todo.pop(0) * block
                value = live * jnp.dot(a_ref[...], n_ref[:, at : at + block], preferred_element_type=F32)
                c_ref[:, at : at + block] = value.astype(BF16)
                ct_ref[at : at + block, :] = value.T.astype(BF16)

    def later_product(half, s):
        start = pl.multiple_of((half * nz + s) * group, group)
        return jnp.dot(ct_ref[pl.ds(start, group), :], pb_ref[...], preferred_element_type=F32)

    groups = [(h, s) for h in range(CORES) for s in range(nz)]

    def rows_of(h, s):
        at = (h * nz + s) * group
        return slice(at, at + group)

    u_norm = jnp.sqrt(all_reduce(0, first_product, sq, form_c) + FLOOR_SQ)
    form_c(len(todo))
    for h, s in groups:
        ft_ref[:, rows_of(h, s)] = flat(full[h, s]).T.astype(BF16)
    inverse = 1.0 / u_norm
    total = jnp.zeros((1, cols), F32)
    for at in range(0, width, block):
        raw = jnp.dot(ft_ref[...], n_ref[:, at : at + block], preferred_element_type=F32).T * inverse
        vecs_ref[0, at : at + block] = raw
        total = total + jnp.sum(raw * raw, axis=0, keepdims=True)
    v_norm = jnp.sqrt(total + FLOOR_SQ)

    def normalise(at_vec, norm):
        scale = 1.0 / norm
        for at in range(0, width, block):
            value = vecs_ref[at_vec, at : at + block] * scale
            vecs_ref[at_vec, at : at + block] = value
            vb_ref[at : at + block] = value.astype(BF16)

    normalise(0, v_norm)
    phi_bar = u_norm
    rho_bar = v_norm
    start_norm = u_norm
    search = [jnp.ones((1, cols), F32)]
    coeffs = [jnp.zeros((1, cols), F32)]

    def project(v_norm, u_norm):
        residue = jnp.dot(c_ref[...], vb_ref[...], preferred_element_type=F32) - left_ref[...] * (v_norm / u_norm)
        left_ref[...] = residue
        pb_ref[...] = residue.astype(BF16)
        return jnp.sum(residue * residue, axis=0, keepdims=True)

    for turn in range(ITERS - 1):
        sq = project(v_norm, u_norm)
        u_norm = jnp.sqrt(all_reduce(turn + 1, later_product, sq, lambda times: None) + FLOOR_SQ)
        inverse = 1.0 / u_norm
        total = jnp.zeros((1, cols), F32)
        for h, s in groups:
            raw = flat(full[h, s]) * inverse - u_norm * vecs_ref[turn, rows_of(h, s)]
            vecs_ref[turn + 1, rows_of(h, s)] = raw
            total = total + jnp.sum(raw * raw, axis=0, keepdims=True)
        v_norm = jnp.sqrt(total + FLOOR_SQ)
        normalise(turn + 1, v_norm)
        radius = jnp.sqrt(rho_bar * rho_bar + u_norm * u_norm)
        cosine = rho_bar / radius
        sine = u_norm / radius
        coupling = sine * v_norm
        rho_bar = -cosine * v_norm
        step = cosine * phi_bar / radius
        phi_bar = sine * phi_bar
        coeffs = [c + step * p for c, p in zip(coeffs, search)] + [jnp.zeros((1, cols), F32)]
        search = [-(coupling / radius) * p for p in search] + [jnp.ones((1, cols), F32)]

    squares = Squares(ITERS, project(v_norm, u_norm))
    squares.send_core()
    shift = lax.rem(cols - z * own_cols, cols)
    for at in range(0, width, block):
        known = sum(c * vecs_ref[i, at : at + block] for i, c in enumerate(coeffs))
        along = sum(p * vecs_ref[i, at : at + block] for i, p in enumerate(search))
        known = pltpu.roll(known, shift, 1)
        along = pltpu.roll(along, shift, 1)
        vecs_ref[0, at : at + block] = known
        vecs_ref[1, at : at + block] = along
        w_ref[at : at + block, :cols] = known.astype(BF16)
        w_ref[at : at + block, cols:] = along.astype(BF16)

    def form_solution(first, last):
        for at in range(first, last, block):
            nw_ref[at : at + block] = jnp.dot(
                n_ref[at : at + block, :], w_ref[...], preferred_element_type=F32
            )

    squares.send_xy()
    form_solution(0, width // 2)
    squares.send_z()
    form_solution(width // 2, width)
    u_norm = jnp.sqrt(squares.finish() + FLOOR_SQ)
    radius = jnp.sqrt(rho_bar * rho_bar + u_norm * u_norm)
    step = rho_bar / radius * phi_bar / radius
    ratio = u_norm / radius * phi_bar / start_norm
    step = pltpu.roll(jnp.broadcast_to(step, (8, cols)), shift, 1)[0:1]
    ratio_ref[...] = pltpu.roll(jnp.broadcast_to(ratio, (8, cols)), shift, 1)[0:1, :own_cols]
    for at in range(0, width, block):
        coef_ref[at : at + block] = (vecs_ref[0, at : at + block] + step * vecs_ref[1, at : at + block])[:, :own_cols]
        sol_ref[at : at + block] = (
            nw_ref[at : at + block, :cols] + step * nw_ref[at : at + block, cols:]
        )[:, :own_cols]


def shards(nrows, nz, matrix, right_side, precond, row_counts):
    local, width = matrix.shape
    cols = right_side.shape[1]
    nxy = nrows // CORES
    chunk = width // (nrows * nz)
    own = cols // nz
    turns = ITERS + 1
    vmem = pltpu.VMEM
    dma = pltpu.SemaphoreType.DMA
    sol, coef, ratio = pl.pallas_call(
        functools.partial(body, nxy, nz),
        out_shape=(
            jax.ShapeDtypeStruct((width, own), F32),
            jax.ShapeDtypeStruct((width, own), F32),
            jax.ShapeDtypeStruct((1, own), F32),
        ),
        in_specs=[
            pl.BlockSpec(memory_space=pltpu.SMEM),
            pl.BlockSpec(memory_space=pl.ANY),
            pl.BlockSpec(memory_space=vmem),
            pl.BlockSpec(memory_space=pl.ANY),
        ],
        out_specs=[pl.BlockSpec(memory_space=vmem)] * 3,
        scratch_shapes=[
            vmem((local, width), BF16),
            vmem((width, width), BF16),
            vmem((local, width), BF16),
            vmem((width, local), BF16),
            vmem((local, cols), F32),
            vmem((ITERS, width, cols), F32),
            vmem((local, cols), BF16),
            vmem((width, cols), BF16),
            vmem((cols, width), BF16),
            vmem((width, 2 * cols), BF16),
            vmem((width, 2 * cols), F32),
            vmem((nz, nxy, chunk, cols), BF16),
            vmem((nz, nxy, chunk, cols), BF16),
            vmem((nz, nxy, chunk, cols), F32),
            vmem((nz, nxy, chunk, cols), BF16),
            vmem((nz, nxy - 1, chunk, cols), BF16),
            vmem((nz - 1, chunk, cols), BF16),
            vmem((nz - 1, chunk, cols), BF16),
            vmem((CORES, nz, nxy, chunk, cols), BF16),
            vmem((turns, 3, 8, cols), F32),
            vmem((turns, 8, cols), F32),
            vmem((turns, nxy, 8, cols), F32),
            vmem((turns, nz, 8, cols), F32),
            dma((2,)),
            dma((nz,)), dma((nz,)),
            dma((nz, nxy - 1)), dma((nz, nxy - 1)),
            dma((nz - 1,)), dma((nz - 1,)),
            dma((nz - 1,)), dma((nz - 1,)),
            dma((nz, nxy - 1)), dma((nz, nxy - 1)),
            dma((nz,)), dma((nz,)),
            dma((turns,)), dma((turns,)),
            dma((turns, nxy - 1)), dma((turns, nxy - 1)),
            dma((turns, nz - 1)), dma((turns, nz - 1)),
        ],
        compiler_params=pltpu.CompilerParams(
            collective_id=0, has_side_effects=True, vmem_limit_bytes=60 * 1024 * 1024
        ),
    )(row_counts, matrix, right_side, precond)
    return (sol, coef, ratio[0])


def solution(mesh):
    return jax.shard_map(
        functools.partial(shards, mesh.shape["rows"], mesh.shape["grp"]),
        mesh=mesh,
        in_specs=(P(("rows", "grp"), None), P(("rows", "grp"), None), P(), P(("rows", "grp"))),
        out_specs=(P(None, "grp"), P(None, "grp"), P("grp")),
        check_vma=False,
    )
```

time: 478 us -> 85.4 us (0.18)
  waiting for transfers between devices: 278 us -> 0 us
  blocking collectives: 127 us -> 0 us
  Pallas kernels: 0 us -> 78.2 us
  matrix products: 49 us -> 0 us
  between operations: 15.1 us -> 1.29 us
    psum x3 -> x0, waiting for transfers between devices: 166 us -> none  [reduce_cols(): return lax.psum((shared, shared_sq), 'rows')]
    all_gather x6 -> x0, blocking collectives: 79.2 us -> none  [the longest x3 44.6 us: share_cols(): pushed = lax.all_gather(pushed, 'grp', axis=1, tiled=True)]
    pallas_call x0 -> x1, Pallas kernels: none -> 78.2 us  [shards(): pl.pallas_call(functools.partial(body, nxy, nz), out_shape=(jax.ShapeDtyp...]
    unnamed x14 -> x0, waiting for transfers between devices: 66.2 us -> none
    dot_general x13 -> x0, matrix products: 49 us -> none  [the longest x3 18 us: share_cols(): jnp.dot(precond, right_vec.astype(jnp.bfloat16), preferred_element_type=j...]
    psum x4 -> x0, blocking collectives: 47.4 us -> none  [reduce_cols(): return lax.psum((shared, shared_sq), 'rows')]
    reduce_scatter x3 -> x0, waiting for transfers between devices: 45.3 us -> none  [reduce_cols(): lax.psum_scatter(partial_value, 'grp', scatter_dimension=1, tiled=True)]
  transfers between devices with their start and end apart: 10 -> 0, of which waited for: 10 -> 0; matrix products, arithmetic and copies ran while one was open for 2% -> 0% of each run, Pallas kernels for 0% -> 0%
where the time goes in v1:
time: 85.4 us; the launch traced here: 85.2 us
  Pallas kernels  78.2 us (92%)
  local copies, waits for them, and re-layouts  5.62 us (7%)
  between operations  1.29 us (2%)
    pallas_call x1, Pallas kernels, shards(): pl.pallas_call(functools.partial(body, nxy, nz), out_shape=(jax.ShapeDtyp...  78.2 us
    unnamed x3, local copies, waits for them, and re-layouts  5.62 us

profile of v1, /device:TPU:0, one launch (start us, length us, event | category | flops | bytes accessed | tf_op | source)
XLA Modules:
  0.0 85.2 jit_solution(12295159109675273282)
XLA Ops:
  1.3 78.2 %shard_map.67 = (f32[2048,32]{1,0:T(8,128)}, f32[2048,32]{1,0:T(8,128)}, f32[1,32]{1,0:T(1,128)}) custom-call(s32[1]{0:T(128)S(6)} %copy.10.count_ref, bf16[512,2048]{1,0:T(8,128)(2,1)} %a_hbm.1, bf16[512,128]{1,0:T(8,128)(2,1)} %b_ref.1, bf16[2048,2048]{1,0:T(8,128)(2,1)} %n_hbm.1), custom_call_target="tpu_custom_call" | custom-call | tf_op jit(solution)/shard_map/pallas_call | solution.py:333
  79.5 2.2 %copy.7 = f32[2048,32]{0,1:T(8,128)} copy(f32[2048,32]{1,0:T(8,128)} %get-tuple-element.9) | data formatting | bytes 524288
  81.8 2.2 %copy.8 = f32[2048,32]{0,1:T(8,128)} copy(f32[2048,32]{1,0:T(8,128)} %get-tuple-element.10) | data formatting | bytes 524288
  84.0 1.1 %copy.11 = f32[32]{0:T(128)} copy(f32[32]{0:T(128)} %bitcast.1) | data formatting | bytes 256

commit v2 on v1

v2 whole, which is shorter than its diff:
```python
import functools

import jax
import jax.numpy as jnp
from jax import lax
from jax.experimental import pallas as pl
from jax.experimental.pallas import tpu as pltpu
from jax.sharding import PartitionSpec as P

ITERS = 3
CORES = 2
FLOOR_SQ = 0.01
F32 = jnp.float32
BF16 = jnp.bfloat16
MESH = pl.DeviceIdType.MESH


def body(
    nrows, nz,
    count_ref, a_hbm, b_hbm, n_hbm,
    sol_ref, coef_ref, ratio_ref,
    a_ref, b_ref, n_ref, c_ref, ct_ref, left_ref, vecs_ref, pb_ref, acc_ref, pull_ref, norms_ref,
    w_ref, flip_ref, nw_ref, step_ref,
    tx0, rx0, hbuf, tx1, rx1, tx2, rx2, full,
    sqtx, sqrx1, sqrx2,
    load_sem, s0, r0, s1, r1, s2, r2, gs2, gr2, gs1, gr1, gs0, gr0,
    qs1, qr1, qs2, qr2,
):
    row = lax.axis_index("rows")
    z = lax.axis_index("grp")
    core = lax.rem(row, CORES)
    xy = row // CORES
    other = 1 - core
    local, width = a_ref.shape
    cols = b_ref.shape[1]
    chunk = full.shape[3]
    nxy = nrows // CORES
    group = nxy * chunk
    own_cols = cols // nz

    def xy_peer(k):
        return lax.rem(xy + k, nxy)

    def z_peer(k):
        return lax.rem(z + k, nz)

    def row_id(at):
        return {"rows": at * CORES + core}

    core_id = {"rows": xy * CORES + other}

    def load_half(half, at):
        span = pl.ds(pl.multiple_of(half * (width // CORES), width // CORES), width // CORES)
        return pltpu.make_async_copy(a_hbm.at[:, span], a_ref.at[:, span], load_sem.at[at])

    load_b = pltpu.make_async_copy(b_hbm, b_ref, load_sem.at[3])
    load_other = load_half(other, 0)
    load_own = load_half(core, 1)
    load_n = pltpu.make_async_copy(n_hbm, n_ref, load_sem.at[2])
    load_b.start()
    load_other.start()
    load_own.start()
    load_n.start()

    barrier = pltpu.get_barrier_semaphore()
    for k in range(1, nrows):
        pl.semaphore_signal(barrier, inc=1, device_id={"rows": lax.rem(row + k, nrows)}, device_id_type=MESH)
    for k in range(1, nz):
        pl.semaphore_signal(barrier, inc=1, device_id={"grp": z_peer(k)}, device_id_type=MESH)

    def remote(src, dst, ssem, rsem, to):
        copy = pltpu.make_async_remote_copy(
            src_ref=src, dst_ref=dst, send_sem=ssem, recv_sem=rsem, device_id=to, device_id_type=MESH
        )
        copy.start()
        return copy

    def flat(value):
        return value.astype(F32).reshape(-1, cols)

    def pieces(value):
        return value.reshape(-1, chunk, cols).astype(BF16)

    class Squares:
        def __init__(self, turn, local_sq):
            self.turn = turn
            self.total = jnp.broadcast_to(local_sq, (8, cols))
            self.sent = []

        def send_rows(self):
            sqtx[self.turn, 0] = self.total
            sqrx1[self.turn, row] = self.total
            self.now = [
                remote(
                    sqtx.at[self.turn, 0], sqrx1.at[self.turn, row],
                    qs1.at[self.turn, k - 1], qr1.at[self.turn, k - 1],
                    {"rows": lax.rem(row + k, nrows)},
                )
                for k in range(1, nrows)
            ]

        def send_z(self):
            for copy in self.now:
                copy.wait_recv()
            self.sent += self.now
            self.total = sum(sqrx1[self.turn, at] for at in range(nrows))
            sqtx[self.turn, 1] = self.total
            sqrx2[self.turn, z] = self.total
            self.now = [
                remote(sqtx.at[self.turn, 1], sqrx2.at[self.turn, z], qs2.at[self.turn, k - 1], qr2.at[self.turn, k - 1], {"grp": z_peer(k)})
                for k in range(1, nz)
            ]

        def finish(self):
            for copy in self.now:
                copy.wait_recv()
            self.sent += self.now
            self.total = sum(sqrx2[self.turn, at] for at in range(nz))
            for copy in self.sent:
                copy.wait_send()
            return self.total[0:1]

    def all_reduce(turn, product, local_sq, filler, consume):
        order = list(range(1, nz)) + [0]
        sends = []
        core_copies = {}
        for d in order:
            s = z_peer(d)
            tx0[s] = pieces(product(other, s))
            if turn == 0 and d == order[0]:
                pl.semaphore_wait(barrier, nrows + nz - 2)
            core_copies[d] = remote(tx0.at[s], rx0.at[s], s0.at[d], r0.at[d], core_id)
        squares = Squares(turn, local_sq)
        squares.send_rows()
        if turn == 0:
            load_own.wait()
        for d in order:
            s = z_peer(d)
            hbuf[s] = product(core, s).reshape(nxy, chunk, cols)
        xy_copies = {}
        for d in order:
            s = z_peer(d)
            core_copies[d].wait_recv()
            total = hbuf[s] + rx0[s].astype(F32)
            hbuf[s] = total
            tx1[s] = total.astype(BF16)
            for k in range(1, nxy):
                at = xy_peer(k)
                xy_copies[d, k] = remote(
                    tx1.at[s, at], rx1.at[d, k - 1], s1.at[d, k - 1], r1.at[d, k - 1], row_id(at)
                )
        filler(2)
        z_copies = {}
        for d in order:
            s = z_peer(d)
            part = hbuf[s, xy]
            for k in range(1, nxy):
                xy_copies[d, k].wait_recv()
                part = part + rx1[d, k - 1].astype(F32)
            if d:
                tx2[d - 1] = part.astype(BF16)
                z_copies[d] = remote(
                    tx2.at[d - 1], rx2.at[d - 1], s2.at[d - 1], r2.at[d - 1], {"grp": s}
                )
        squares.send_z()
        filler(2)
        for d in range(1, nz):
            z_copies[d].wait_recv()
            part = part + rx2[d - 1].astype(F32)
        full[core, z, xy] = part.astype(BF16)
        gather_z = [
            remote(full.at[core, z, xy], full.at[core, z, xy], gs2.at[d - 1], gr2.at[d - 1], {"grp": z_peer(d)})
            for d in range(1, nz)
        ]
        gather_xy = {}

        def spread(d, zz):
            for k in range(1, nxy):
                gather_xy[d, k] = remote(
                    full.at[core, zz, xy], full.at[core, zz, xy],
                    gs1.at[d, k - 1], gr1.at[d, k - 1], row_id(xy_peer(k)),
                )

        spread(0, z)
        u_norm = jnp.sqrt(squares.finish() + FLOOR_SQ)
        filler(3)
        for d in range(1, nz):
            gather_z[d - 1].wait_recv()
            spread(d, z_peer(nz - d))
        filler(1)
        gather_core = []
        consume = consume(u_norm)
        for d in range(nz):
            zz = z_peer((nz - d) % nz)
            for k in range(1, nxy):
                gather_xy[d, k].wait_recv()
            gather_core.append(
                remote(full.at[core, zz], full.at[core, zz], gs0.at[d], gr0.at[d], core_id)
            )
            consume(core, zz)
            if d:
                gather_core[d - 1].wait_recv()
                consume(other, z_peer((nz - d + 1) % nz))
        gather_core[nz - 1].wait_recv()
        consume(other, z_peer(1 % nz))
        for copies in (core_copies, xy_copies, z_copies, gather_xy):
            for copy in copies.values():
                copy.wait_send()
        for copy in gather_z + gather_core:
            copy.wait_send()
        return u_norm

    live = (lax.broadcasted_iota(jnp.int32, (local, 1), 0) < count_ref[0]).astype(F32)

    load_b.wait()
    residue = live * b_ref[...].astype(F32)
    left_ref[...] = residue
    sq = jnp.sum(residue * residue, axis=0, keepdims=True)
    bt = residue.T.astype(BF16)
    load_other.wait()

    def first_product(half, s):
        start = pl.multiple_of((half * nz + s) * group, group)
        return jnp.dot(bt, a_ref[:, pl.ds(start, group)], preferred_element_type=F32).T

    block = 256
    todo = list(range(width // block))

    def form_c(times):
        if len(todo) == width // block:
            load_n.wait()
        for _ in range(times):
            if todo:
                at = todo.pop(0) * block
                value = live * jnp.dot(a_ref[...], n_ref[:, at : at + block], preferred_element_type=F32)
                c_ref[:, at : at + block] = value.astype(BF16)
                ct_ref[at : at + block, :] = value.T.astype(BF16)

    def later_product(half, s):
        start = pl.multiple_of((half * nz + s) * group, group)
        return jnp.dot(ct_ref[pl.ds(start, group), :], pb_ref[...], preferred_element_type=F32)

    def rows_of(half, s):
        return pl.ds(pl.multiple_of((half * nz + s) * group, group), group)

    def fold(raw):
        return jnp.sum((raw * raw).reshape(-1, 8, cols), axis=0)

    def norm_of(terms):
        total = sum(norms_ref[at] for at in range(terms))
        return jnp.sqrt(jnp.sum(total, axis=0, keepdims=True) + FLOOR_SQ)

    def pull_group(u_norm):
        pull_ref[...] = jnp.zeros_like(pull_ref)

        def consume(half, s):
            turned = flat(full[half, s]).T.astype(BF16)
            pull_ref[...] += jnp.dot(turned, n_ref[rows_of(half, s), :], preferred_element_type=F32)

        return consume

    def advance_group(turn, scale):
        def begin(u_norm):
            inverse = 1.0 / u_norm
            back = u_norm * scale
            acc_ref[...] = jnp.zeros_like(acc_ref)

            def consume(half, s):
                rows = rows_of(half, s)
                raw = flat(full[half, s]) * inverse - back * vecs_ref[turn, rows]
                vecs_ref[turn + 1, rows] = raw
                norms_ref[half * nz + s] = fold(raw)
                acc_ref[...] += jnp.dot(c_ref[:, rows], raw.astype(BF16), preferred_element_type=F32)

            return consume

        return begin

    u_norm = all_reduce(0, first_product, sq, form_c, pull_group)
    form_c(len(todo))
    inverse = 1.0 / u_norm
    acc = None
    for i, at in enumerate(range(0, width, block)):
        raw = pull_ref[:, at : at + block].T * inverse
        vecs_ref[0, at : at + block] = raw
        norms_ref[i] = fold(raw)
        term = jnp.dot(c_ref[:, at : at + block], raw.astype(BF16), preferred_element_type=F32)
        if i:
            acc_ref[...] += term
        else:
            acc_ref[...] = term
    v_norm = norm_of(width // block)
    scales = [1.0 / v_norm]
    phi_bar = u_norm
    rho_bar = v_norm
    start_norm = u_norm
    search = [jnp.ones((1, cols), F32)]
    coeffs = [jnp.zeros((1, cols), F32)]

    def project(v_norm, u_norm):
        residue = acc_ref[...] * (1.0 / v_norm) - left_ref[...] * (v_norm / u_norm)
        left_ref[...] = residue
        pb_ref[...] = residue.astype(BF16)
        return jnp.sum(residue * residue, axis=0, keepdims=True)

    for turn in range(ITERS - 1):
        sq = project(v_norm, u_norm)
        u_norm = all_reduce(
            turn + 1, later_product, sq, lambda times: None, advance_group(turn, scales[turn])
        )
        v_norm = norm_of(CORES * nz)
        scales.append(1.0 / v_norm)
        radius = jnp.sqrt(rho_bar * rho_bar + u_norm * u_norm)
        cosine = rho_bar / radius
        sine = u_norm / radius
        coupling = sine * v_norm
        rho_bar = -cosine * v_norm
        step = cosine * phi_bar / radius
        phi_bar = sine * phi_bar
        coeffs = [c + step * p for c, p in zip(coeffs, search)] + [jnp.zeros((1, cols), F32)]
        search = [-(coupling / radius) * p for p in search] + [jnp.ones((1, cols), F32)]

    squares = Squares(ITERS, project(v_norm, u_norm))
    squares.send_rows()
    coeffs = [c * scale for c, scale in zip(coeffs, scales)]
    search = [p * scale for p, scale in zip(search, scales)]
    for at in range(0, width, block):
        known = sum(c * vecs_ref[i, at : at + block] for i, c in enumerate(coeffs))
        along = sum(p * vecs_ref[i, at : at + block] for i, p in enumerate(search))
        flip_ref[:cols, at : at + block] = known.T
        flip_ref[cols:, at : at + block] = along.T
        w_ref[at : at + block, :cols] = known.astype(BF16)
        w_ref[at : at + block, cols:] = along.astype(BF16)

    def form_solution(first, last):
        for at in range(first, last, block):
            nw_ref[:, at : at + block] = jnp.dot(
                n_ref[at : at + block, :], w_ref[...], preferred_element_type=F32
            ).T

    squares.send_z()
    form_solution(0, width)
    u_norm = jnp.sqrt(squares.finish() + FLOOR_SQ)
    radius = jnp.sqrt(rho_bar * rho_bar + u_norm * u_norm)
    step = rho_bar / radius * phi_bar / radius
    ratio = u_norm / radius * phi_bar / start_norm
    shift = lax.rem(cols - z * own_cols, cols)
    ratio_ref[...] = pltpu.roll(jnp.broadcast_to(ratio, (8, cols)), shift, 1)[0:1, :own_cols]
    step_ref[...] = jnp.broadcast_to(step, (cols, cols)).T
    mine = pl.ds(pl.multiple_of(z * own_cols, own_cols), own_cols)
    mine_too = pl.ds(pl.multiple_of(cols + z * own_cols, own_cols), own_cols)
    step = step_ref[mine, :]
    for at in range(0, width, cols):
        span = slice(at, at + cols)
        coef_ref[:, span] = flip_ref[mine, span] + step * flip_ref[mine_too, span]
        sol_ref[:, span] = nw_ref[mine, span] + step * nw_ref[mine_too, span]


def shards(nrows, nz, matrix, right_side, precond, row_counts):
    local, width = matrix.shape
    cols = right_side.shape[1]
    nxy = nrows // CORES
    chunk = width // (nrows * nz)
    own = cols // nz
    turns = ITERS + 1
    vmem = pltpu.VMEM
    dma = pltpu.SemaphoreType.DMA
    sol, coef, ratio = pl.pallas_call(
        functools.partial(body, nrows, nz),
        out_shape=(
            jax.ShapeDtypeStruct((own, width), F32),
            jax.ShapeDtypeStruct((own, width), F32),
            jax.ShapeDtypeStruct((1, own), F32),
        ),
        in_specs=[
            pl.BlockSpec(memory_space=pltpu.SMEM),
            pl.BlockSpec(memory_space=pl.ANY),
            pl.BlockSpec(memory_space=pl.ANY),
            pl.BlockSpec(memory_space=pl.ANY),
        ],
        out_specs=[pl.BlockSpec(memory_space=vmem)] * 3,
        scratch_shapes=[
            vmem((local, width), BF16),
            vmem((local, cols), BF16),
            vmem((width, width), BF16),
            vmem((local, width), BF16),
            vmem((width, local), BF16),
            vmem((local, cols), F32),
            vmem((ITERS, width, cols), F32),
            vmem((local, cols), BF16),
            vmem((local, cols), F32),
            vmem((cols, width), F32),
            vmem((max(CORES * nz, width // 256), 8, cols), F32),
            vmem((width, 2 * cols), BF16),
            vmem((2 * cols, width), F32),
            vmem((2 * cols, width), F32),
            vmem((cols, cols), F32),
            vmem((nz, nxy, chunk, cols), BF16),
            vmem((nz, nxy, chunk, cols), BF16),
            vmem((nz, nxy, chunk, cols), F32),
            vmem((nz, nxy, chunk, cols), BF16),
            vmem((nz, nxy - 1, chunk, cols), BF16),
            vmem((nz - 1, chunk, cols), BF16),
            vmem((nz - 1, chunk, cols), BF16),
            vmem((CORES, nz, nxy, chunk, cols), BF16),
            vmem((turns, 2, 8, cols), F32),
            vmem((turns, nrows, 8, cols), F32),
            vmem((turns, nz, 8, cols), F32),
            dma((4,)),
            dma((nz,)), dma((nz,)),
            dma((nz, nxy - 1)), dma((nz, nxy - 1)),
            dma((nz - 1,)), dma((nz - 1,)),
            dma((nz - 1,)), dma((nz - 1,)),
            dma((nz, nxy - 1)), dma((nz, nxy - 1)),
            dma((nz,)), dma((nz,)),
            dma((turns, nrows - 1)), dma((turns, nrows - 1)),
            dma((turns, nz - 1)), dma((turns, nz - 1)),
        ],
        compiler_params=pltpu.CompilerParams(
            collective_id=0, has_side_effects=True, vmem_limit_bytes=60 * 1024 * 1024
        ),
    )(row_counts, matrix, right_side, precond)
    return (sol.T, coef.T, ratio[0])


def solution(mesh):
    return jax.shard_map(
        functools.partial(shards, mesh.shape["rows"], mesh.shape["grp"]),
        mesh=mesh,
        in_specs=(P(("rows", "grp"), None), P(("rows", "grp"), None), P(), P(("rows", "grp"))),
        out_specs=(P(None, "grp"), P(None, "grp"), P("grp")),
        check_vma=False,
    )
```

time: 85.4 us -> 81 us (0.948)
  Pallas kernels: 78.2 us -> 75 us
  local copies, waits for them, and re-layouts: 5.62 us -> 4.44 us
    pallas_call x1, Pallas kernels: 78.2 us -> 75 us  [shards(): pl.pallas_call(functools.partial(body, nrows, nz), out_shape=(jax.ShapeDt...]
    unnamed x3, local copies, waits for them, and re-layouts: 5.62 us -> 4.44 us
where the time goes in v2:
time: 81 us; the launch traced here: 80.8 us
  Pallas kernels  75 us (93%)
  local copies, waits for them, and re-layouts  4.44 us (5%)
  between operations  1.29 us (2%)
    pallas_call x1, Pallas kernels, shards(): pl.pallas_call(functools.partial(body, nrows, nz), out_shape=(jax.ShapeDt...  75 us
    unnamed x3, local copies, waits for them, and re-layouts  4.44 us

profile of v2, /device:TPU:0, one launch (start us, length us, event | category | flops | bytes accessed | tf_op | source)
XLA Modules:
  0.0 80.8 jit_solution(3809326213861968281)
XLA Ops:
  1.3 75.0 %shard_map.67 = (f32[32,2048]{1,0:T(8,128)}, f32[32,2048]{1,0:T(8,128)}, f32[1,32]{1,0:T(1,128)}) custom-call(s32[1]{0:T(128)S(6)} %copy.10.count_ref, bf16[512,2048]{1,0:T(8,128)(2,1)} %a_hbm.1, bf16[512,128]{1,0:T(8,128)(2,1)} %b_hbm.1, bf16[2048,2048]{1,0:T(8,128)(2,1)} %n_hbm.1), custom_call_target="tpu_custom_call" | custom-call | tf_op jit(solution)/shard_map/pallas_call | solution.py:368
  76.3 1.7 %copy.11 = f32[2048,32]{0,1:T(8,128)} copy(f32[2048,32]{0,1:T(8,128)} %bitcast.4) | data formatting | bytes 524288
  78.0 1.7 %copy.12 = f32[2048,32]{0,1:T(8,128)} copy(f32[2048,32]{0,1:T(8,128)} %bitcast.3) | data formatting | bytes 524288
  79.7 1.1 %copy.13 = f32[32]{0:T(128)} copy(f32[32]{0:T(128)} %bitcast.5) | data formatting | bytes 256

commit v3 on v2

--- a/solution.py
+++ b/solution.py
@@ -18,7 +18,7 @@
 def body(
     nrows, nz,
     count_ref, a_hbm, b_hbm, n_hbm,
-    sol_ref, coef_ref, ratio_ref,
+    both_ref, ratio_ref,
     a_ref, b_ref, n_ref, c_ref, ct_ref, left_ref, vecs_ref, pb_ref, acc_ref, pull_ref, norms_ref,
     w_ref, flip_ref, nw_ref, step_ref,
     tx0, rx0, hbuf, tx1, rx1, tx2, rx2, full,
@@ -60,7 +60,6 @@
     load_b.start()
     load_other.start()
     load_own.start()
-    load_n.start()
 
     barrier = pltpu.get_barrier_semaphore()
     for k in range(1, nrows):
@@ -134,6 +133,7 @@
         squares.send_rows()
         if turn == 0:
             load_own.wait()
+            load_n.start()
         for d in order:
             s = z_peer(d)
             hbuf[s] = product(core, s).reshape(nxy, chunk, cols)
@@ -198,11 +198,12 @@
                 remote(full.at[core, zz], full.at[core, zz], gs0.at[d], gr0.at[d], core_id)
             )
             consume(core, zz)
-            if d:
+            if d and turn:
                 gather_core[d - 1].wait_recv()
                 consume(other, z_peer((nz - d + 1) % nz))
-        gather_core[nz - 1].wait_recv()
-        consume(other, z_peer(1 % nz))
+        for d in range(nz - 1 if turn else 0, nz):
+            gather_core[d].wait_recv()
+            consume(other, z_peer((nz - d) % nz))
         for copies in (core_copies, xy_copies, z_copies, gather_xy):
             for copy in copies.values():
                 copy.wait_send()
@@ -352,8 +353,28 @@
     step = step_ref[mine, :]
     for at in range(0, width, cols):
         span = slice(at, at + cols)
-        coef_ref[:, span] = flip_ref[mine, span] + step * flip_ref[mine_too, span]
-        sol_ref[:, span] = nw_ref[mine, span] + step * nw_ref[mine_too, span]
+        both_ref[own_cols:, span] = flip_ref[mine, span] + step * flip_ref[mine_too, span]
+        both_ref[:own_cols, span] = nw_ref[mine, span] + step * nw_ref[mine_too, span]
+
+
+def hand_over(both_hbm, ratio_in, sol_hbm, coef_hbm, ratio_out, held, in_sem, out_sem):
+    own = sol_hbm.shape[0]
+    halves = [pl.ds(0, own), pl.ds(own, own)]
+    inward = [
+        pltpu.make_async_copy(both_hbm.at[half], held.at[half], in_sem.at[i]) for i, half in enumerate(halves)
+    ]
+    outward = [
+        pltpu.make_async_copy(held.at[half], to, out_sem.at[i])
+        for i, (half, to) in enumerate(zip(halves, (sol_hbm, coef_hbm)))
+    ]
+    for copy in inward:
+        copy.start()
+    ratio_out[...] = ratio_in[...]
+    for first, second in zip(inward, outward):
+        first.wait()
+        second.start()
+    for copy in outward:
+        copy.wait()
 
 
 def shards(nrows, nz, matrix, right_side, precond, row_counts):
@@ -365,11 +386,10 @@
     turns = ITERS + 1
     vmem = pltpu.VMEM
     dma = pltpu.SemaphoreType.DMA
-    sol, coef, ratio = pl.pallas_call(
+    both, ratio = pl.pallas_call(
         functools.partial(body, nrows, nz),
         out_shape=(
-            jax.ShapeDtypeStruct((own, width), F32),
-            jax.ShapeDtypeStruct((own, width), F32),
+            jax.ShapeDtypeStruct((2 * own, width), F32),
             jax.ShapeDtypeStruct((1, own), F32),
         ),
         in_specs=[
@@ -378,7 +398,7 @@
             pl.BlockSpec(memory_space=pl.ANY),
             pl.BlockSpec(memory_space=pl.ANY),
         ],
-        out_specs=[pl.BlockSpec(memory_space=vmem)] * 3,
+        out_specs=[pl.BlockSpec(memory_space=vmem)] * 2,
         scratch_shapes=[
             vmem((local, width), BF16),
             vmem((local, cols), BF16),
@@ -420,6 +440,22 @@
             collective_id=0, has_side_effects=True, vmem_limit_bytes=60 * 1024 * 1024
         ),
     )(row_counts, matrix, right_side, precond)
+    sol, coef, ratio = pl.pallas_call(
+        hand_over,
+        out_shape=(
+            jax.ShapeDtypeStruct((own, width), F32),
+            jax.ShapeDtypeStruct((own, width), F32),
+            jax.ShapeDtypeStruct((1, own), F32),
+        ),
+        in_specs=[pl.BlockSpec(memory_space=pl.ANY), pl.BlockSpec(memory_space=vmem)],
+        out_specs=[
+            pl.BlockSpec(memory_space=pl.ANY),
+            pl.BlockSpec(memory_space=pl.ANY),
+            pl.BlockSpec(memory_space=vmem),
+        ],
+        scratch_shapes=[vmem((2 * own, width), F32), dma((2,)), dma((2,))],
+        compiler_params=pltpu.CompilerParams(vmem_limit_bytes=60 * 1024 * 1024),
+    )(both, ratio)
     return (sol.T, coef.T, ratio[0])
 
 

time: 81 us -> 78.8 us (0.973)
  local copies, waits for them, and re-layouts: 4.44 us -> 0 us
  Pallas kernels: 75 us -> 77.1 us
    unnamed x3 -> x0, local copies, waits for them, and re-layouts: 4.44 us -> none
    pallas_call x0 -> x1, Pallas kernels: none -> 2.95 us  [shards(): pl.pallas_call(hand_over, out_shape=(jax.ShapeDtypeStruct((own, width), F...]
    pallas_call x1, Pallas kernels: 75 us -> 74.2 us  [shards(): pl.pallas_call(functools.partial(body, nrows, nz), out_shape=(jax.ShapeDt...]
where the time goes in v3:
time: 78.8 us; the launch traced here: 78.6 us
  Pallas kernels  77.1 us (98%)
  between operations  1.45 us (2%)
    pallas_call x1, Pallas kernels, shards(): pl.pallas_call(functools.partial(body, nrows, nz), out_shape=(jax.ShapeDt...  74.2 us
    pallas_call x1, Pallas kernels, shards(): pl.pallas_call(hand_over, out_shape=(jax.ShapeDtypeStruct((own, width), F...  2.95 us

profile of v3, /device:TPU:0, one launch (start us, length us, event | category | flops | bytes accessed | tf_op | source)
XLA Modules:
  0.0 78.6 jit_solution(11643381299439002660)
XLA Ops:
  1.3 74.2 %shard_map.67 = (f32[64,2048]{1,0:T(8,128)}, f32[1,32]{1,0:T(1,128)}) custom-call(s32[1]{0:T(128)S(6)} %copy.7.count_ref, bf16[512,2048]{1,0:T(8,128)(2,1)} %a_hbm.1, bf16[512,128]{1,0:T(8,128)(2,1)} %b_hbm.1, bf16[2048,2048]{1,0:T(8,128)(2,1)} %n_hbm.1), custom_call_target="tpu_custom_call" | custom-call | tf_op jit(solution)/shard_map/pallas_call | solution.py:389
  75.5 3.0 %shard_map.68 = (f32[32,2048]{1,0:T(8,128)}, f32[32,2048]{1,0:T(8,128)}, f32[1,32]{1,0:T(1,128)}) custom-call(f32[64,2048]{1,0:T(8,128)} %get-tuple-element.8.both_hbm, f32[1,32]{1,0:T(1,128)} %get-tuple-element.9.ratio_in), custom_call_target="tpu_custom_call" | custom-call | tf_op jit(solution)/shard_map/pallas_call | solution.py:443
